TPU v7x, 128 devices: a whole 4x4x4 slice. The times are simulated.
128 devices in a mesh: rep: 8 (over z, core), ep: 16 (over x, y).
Axes of the slice: x: 4, y: 4, z: 4, core: 2. Of those that a mesh axis runs over, the one named last changes fastest.
Arguments:
- latent_pages: bfloat16 [6144, 36864], P(('rep', 'ep')), may hold values from -4 to 4
- queries: bfloat16 [1024, 147456], P(('rep', 'ep')), may hold values from -4 to 4
- residual: bfloat16 [1024, 14336], P(('rep', 'ep')), may hold values from -6 to 6
- page_count: int32 [8, 16, 8], P(None, 'ep'), may hold values from 1 to 12, 48 in all within a row
- last_fill: int32 [8, 16, 8], P(None, 'ep'), may hold values from 4 to 64
- page_order: int32 [128, 48], P(('rep', 'ep')), may hold values from 0 to 47, each once within a row
- shed_slots: int32 [8, 16, 2], P(None, 'ep'), may hold values from 0 to 7, as said below
- shed_shift: int32 [16, 2], P('ep'), may hold values from 1 to 7
- expert_ids: int32 [4096, 8], P(('rep', 'ep')), may hold values from 0 to 127, all different within a row; in each aligned block of 32 rows (0 to 31, 32 to 63, ...) at most 4 rows name the same one
- gate_weight: float32 [4096, 8], P(('rep', 'ep')), may hold values from 0.05 to 0.5
- expert_home: int32 [128], replicated, may hold values from 0 to 127, each once
- norm_gain: float32 [3584], replicated, may hold values from 0.1 to 1.9
- value_up: bfloat16 [64, 512, 128], P('ep'), may hold values from -0.59765625 to 0.59765625
- out_weight: bfloat16 [8192, 3584], P('ep'), may hold values from -0.14941406 to 0.14941406
- expert_in: bfloat16 [128, 3584, 1024], P(('rep', 'ep')), may hold values from -0.09375 to 0.09375
- expert_out: bfloat16 [128, 1024, 3584], P(('rep', 'ep')), may hold values from -0.1875 to 0.1875
Outputs:
- attn_proj: bfloat16 [1024, 14336], P(('rep', 'ep'))
- layer_out: bfloat16 [1024, 14336], P(('rep', 'ep'))
Inputs may be any that keep to these rules, and one draw needn't show every extreme that they name: `shed_slots`: for each device, 2 different slots. `expert_ids`: each row names 8 different experts; in the rows of one device no expert is named by more than 4 rows.
All inputs are finite; a program needn't handle non-finite values.
Results may differ from a plain program's by a relative error of at most 0.015.
Values may be sent and summed in bfloat16 or wider, within the bound.
No kernel may reach another device: no remote copies, remote signals or barrier semaphores. Data moves between devices by JAX's collectives and lax.ppermute only.
A program may use at most 192 MiB of HBM per device.

v0:
```python
import jax
import jax.numpy as jnp
from jax import lax
from jax.sharding import Mesh
from jax.sharding import PartitionSpec as P

D = 3584
HEADS = 64
LAT = 512
KVW = 576
VHEAD = 128
TOP = 8
PAGE = 64
SPEC = 4
MAXP = 12
REQ_DEV = 8
PAGES_DEV = 48
EP = ("ep_0", "ep_1")
REP_EP = ("rep", "ep_0", "ep_1")
SCORE_SCALE = 192.0 ** (-0.5)
NORM_EPS = 0.25


def shifted(value, axis, steps):
    count = lax.axis_size(axis)
    pairs = [(source, (source + steps) % count) for source in range(count)]
    return lax.ppermute(value, axis, pairs)


def own_rows_2(terms, axes):
    so_far = terms.astype(jnp.bfloat16)
    for axis in axes:
        so_far = lax.psum_scatter(so_far, axis, scatter_dimension=0, tiled=True)
    return so_far.astype(jnp.float32)


def attend(key_block, query_block, lengths):
    request_count = key_block.shape[0]
    key_rows = key_block.reshape(request_count, MAXP * PAGE, KVW)
    query_rows = query_block.reshape(request_count, SPEC * HEADS, KVW)
    scores = (
        jnp.einsum("rqc,rkc->rqk", query_rows, key_rows, preferred_element_type=jnp.float32)
        * SCORE_SCALE
    )
    position = jnp.arange(MAXP * PAGE, dtype=jnp.int32)
    offset = jnp.arange(SPEC * HEADS, dtype=jnp.int32) // HEADS
    visible_end = lengths[:, None] - SPEC + 1 + offset[None, :]
    visible = position[None, None, :] < visible_end[:, :, None]
    scores = jnp.where(visible, scores, -1e30)
    exponent = jnp.exp(scores - jnp.max(scores, axis=2, keepdims=True))
    probability = (exponent / jnp.sum(exponent, axis=2, keepdims=True)).astype(jnp.bfloat16)
    latent = jnp.einsum(
        "rqk,rkl->rql", probability, key_rows[:, :, :LAT], preferred_element_type=jnp.float32
    )
    return latent.astype(jnp.bfloat16).reshape(request_count, SPEC * HEADS * LAT)


def fill_slots(arrived, picker, present, own_rows):
    return jnp.where(present[:, None], arrived[picker], own_rows)


def per_device(
    latent_pages,
    queries,
    residual,
    page_count,
    last_fill,
    page_order,
    shed_slots,
    shed_shift,
    expert_ids,
    gate_weight,
    expert_home,
    norm_gain,
    value_up,
    out_weight,
    expert_in,
    expert_out,
):
    rep_count = lax.axis_size("rep")
    col_count = lax.axis_size(EP)
    device_count = rep_count * col_count
    replica = lax.axis_index("rep")
    lengths = (page_count[:, 0, :] - 1) * PAGE + last_fill[:, 0, :]
    shed_table = shed_slots[:, 0, :]
    own_counts = page_count[replica, 0, :]
    offsets = jnp.cumsum(own_counts) - own_counts
    page_steps = jnp.arange(MAXP, dtype=jnp.int32)
    positions = jnp.minimum(offsets[:, None] + page_steps[None, :], PAGES_DEV - 1)
    own_keys = latent_pages[page_order[0][positions]].reshape(REQ_DEV, MAXP * PAGE * KVW)
    own_lengths = lengths[replica]
    own_sheds = shed_table[replica]
    shifts = shed_shift[0]
    matches = own_sheds[None, :] == jnp.arange(REQ_DEV, dtype=jnp.int32)[:, None]
    present = jnp.any(matches, axis=1)
    picker = jnp.argmax(matches, axis=1)
    own_latent = attend(own_keys, queries, own_lengths)
    tokens_dev = REQ_DEV * SPEC
    heads_dev = value_up.shape[0]
    token_latent = own_latent.reshape(tokens_dev, HEADS * LAT)
    regrouped = lax.all_to_all(token_latent, EP, split_axis=1, concat_axis=0, tiled=True)
    row_block = regrouped.reshape(tokens_dev * lax.axis_size(EP), heads_dev, LAT)
    lifted = jnp.einsum(
        "thl,hlv->thv", row_block, value_up, preferred_element_type=jnp.float32
    ).astype(jnp.bfloat16)
    branch = own_rows_2(
        jnp.dot(
            lifted.reshape(tokens_dev * lax.axis_size(EP), heads_dev * VHEAD),
            out_weight,
            preferred_element_type=jnp.float32,
        ),
        EP,
    )
    own_branch = branch.astype(jnp.bfloat16).reshape(REQ_DEV, SPEC * D)
    arrived = jnp.concatenate((own_branch[own_sheds], residual[own_sheds]), axis=1)
    for bit_level in range(rep_count.bit_length() - 1):
        moved = shifted(arrived, "rep", 1 << bit_level)
        taking = shifts // (1 << bit_level) % 2 == 1
        arrived = jnp.where(taking[:, None], moved, arrived)
    served_branch = fill_slots(arrived[:, : SPEC * D], picker, present, own_branch)
    served_rest = fill_slots(arrived[:, SPEC * D :], picker, present, residual)
    branch = served_branch.reshape(tokens_dev, D).astype(jnp.float32)
    mixed = served_rest.reshape(tokens_dev, D).astype(jnp.float32) + branch
    square = jnp.mean(mixed * mixed, axis=1, keepdims=True)
    normed = (mixed * lax.rsqrt(square + NORM_EPS) * norm_gain).astype(jnp.bfloat16)
    capacity = max(4, 2 * tokens_dev * TOP // device_count)
    flat_ids = expert_ids.reshape(-1)
    target = expert_home[flat_ids]
    hits = (target[:, None] == jnp.arange(device_count, dtype=jnp.int32)[None, :]).astype(jnp.int32)
    before = jnp.sum((jnp.cumsum(hits, axis=0) - hits) * hits, axis=1)
    slot_index = target * capacity + before
    buffer_rows = jnp.arange(device_count * capacity, dtype=jnp.int32)
    landing = buffer_rows[:, None, None] == slot_index.reshape(tokens_dev, TOP)[None, :, :]
    chooser = jnp.any(landing, axis=2).astype(jnp.bfloat16)
    outgoing_tokens = jnp.dot(chooser, normed, preferred_element_type=jnp.float32).astype(
        jnp.bfloat16
    )
    incoming = lax.all_to_all(
        outgoing_tokens.reshape(device_count, capacity, D),
        REP_EP,
        split_axis=0,
        concat_axis=0,
        tiled=True,
    )
    inner_act = jax.nn.silu(
        jnp.dot(
            incoming.reshape(device_count * capacity, D),
            expert_in[0],
            preferred_element_type=jnp.float32,
        )
    ).astype(jnp.bfloat16)
    outer_out = jnp.dot(inner_act, expert_out[0], preferred_element_type=jnp.float32).astype(
        jnp.bfloat16
    )
    returned = lax.all_to_all(
        outer_out.reshape(device_count, capacity, D),
        REP_EP,
        split_axis=0,
        concat_axis=0,
        tiled=True,
    )
    picked = (
        returned.reshape(device_count * capacity, D)[slot_index]
        .reshape(tokens_dev, TOP, D)
        .astype(jnp.float32)
    )
    moe_sum = jnp.sum(gate_weight[:, :, None] * picked, axis=1)
    attn_proj = served_branch
    layer_out = (mixed + moe_sum).astype(jnp.bfloat16).reshape(REQ_DEV, SPEC * D)
    return (attn_proj, layer_out)


def solution(mesh):
    torus = Mesh(mesh.devices.reshape(mesh.shape["rep"], 4, 4), ("rep", "ep_0", "ep_1"))
    return jax.shard_map(
        per_device,
        mesh=torus,
        in_specs=(
            P(REP_EP, None),
            P(REP_EP, None),
            P(REP_EP, None),
            P(None, EP, None),
            P(None, EP, None),
            P(REP_EP, None),
            P(None, EP, None),
            P(EP, None),
            P(REP_EP, None),
            P(REP_EP, None),
            P(),
            P(),
            P(EP, None, None),
            P(EP, None),
            P(REP_EP, None, None),
            P(REP_EP, None, None),
        ),
        out_specs=(P(REP_EP, None), P(REP_EP, None)),
        check_vma=False,
    )
```

profile of v0, /device:TPU:1, one launch (start us, length us, event | category | flops | bytes accessed | tf_op | source)
XLA Modules:
  0.0 374.2 jit_solution(15845066801113839272)
XLA Ops:
  7.2 0.6 and_select_fusion
  7.8 1.6 fusion.45
  9.3 0.2 reduce-window.18
  9.5 0.7 bitcast_subtract_fusion.1
  10.4 1.6 gather_fusion
  12.0 0.7 reshape.439
  12.7 0.8 copy.40
  13.5 0.7 reshape.420
  14.1 0.7 compare_select_fusion.3
  14.8 0.7 pad_clamp_fusion.1
  15.5 8.1 %gather_fusion.1 = bf16[96,36864]{1,0:T(8,128)(2,1)} fusion(bf16[48,36864]{1,0:T(8,128)(2,1)S(1)} %copy-done, s32[1024]{0:T(1024)S(1)} %get-tuple-element.18), kind=kCustom, calls=%fused_computation.1 | custom fusion | bytes 14156160 | tf_op jit(solution)/shard_map/gather | solution.py:90
  23.6 14.2 %reshape_reshape.4 = bf16[8,768,576]{2,1,0:T(8,128)(2,1)} reshape(bf16[96,36864]{1,0:T(8,128)(2,1)} %gather_fusion.1) | data formatting | bytes 14155776 | tf_op jit(solution)/shard_map/reshape;reshape | solution.py:39
  37.8 2.7 reshape.501
  40.5 3.3 reshape.416
  43.9 10.7 %fusion.51 = (f32[8,256]{1,0:T(8,128)S(1)}, f32[8,256,768]{1,2,0:T(8,128)}) fusion(s32[8,256]{1,0:T(8,128)S(1)} %broadcast_add_fusion.1, bf16[8,768,576]{2,1,0:T(8,128)(2,1)} %reshape_reshape.4, bf16[8,256,576]{2,1,0:T(8,128)(2,1)} %reshape.416), kind=kOutput, calls=%fused_computation.115 | convolution fusion | flops 1819804416 | bytes 15745024 | tf_op jit(solution)/shard_map/sub | solution.py:50
  54.6 7.8 %fusion.18 = bf16[8,256,512]{2,1,0:T(8,128)(2,1)} fusion(bf16[8,768,576]{2,1,0:T(8,128)(2,1)} %reshape_reshape.4, f32[8,256,768]{1,2,0:T(8,128)} %get-tuple-element.16, f32[8,256]{1,0:T(8,128)S(1)} %get-tuple-element.15), kind=kOutput, calls=%fused_computation.32 | convolution fusion | flops 1614807040 | bytes 14688256 | tf_op jit(solution)/shard_map/rqk,rkl->rql/dot_general | solution.py:52
  62.4 3.1 all_to_all.18
  65.5 1.2 copy.36
  66.7 34.7 %all_to_all.26 = bf16[32,16,2048]{2,0,1:T(8,128)(2,1)S(1)} all-to-all(bf16[32,16,2048]{2,0,1:T(8,128)(2,1)S(1)} %copy.36), channel_id=1, replica_groups=mesh['rep'=8,'ep_0'=4,'ep_1'=4] {'ep_0','ep_1'}, dimensions={1} | all-to-all | bytes 4194304 | tf_op jit(solution)/shard_map/all_to_all | solution.py:101
  101.3 2.8 reshape.417
  104.1 2.6 fusion.23
  106.8 3.9 %convolution_convert_fusion.1 = bf16[512,3584]{1,0:T(8,128)(2,1)} fusion(bf16[512,512]{0,1:T(8,128)(2,1)S(1)} %bitcast.103, bf16[512,3584]{1,0:T(8,128)(2,1)S(1)} %copy-done.4), kind=kOutput, calls=%fused_computation.21 | convolution fusion | flops 1880883200 | bytes 7864320 | tf_op jit(solution)/shard_map/dot_general | solution.py:107
  110.7 43.1 %reduce-scatter.3.cloned.1.call-done = bf16[128,3584]{1,0:T(8,128)(2,1)} async-done(((bf16[512,3584]{1,0:T(8,128)(2,1)}), bf16[128,3584]{1,0:T(8,128)(2,1)}) %reduce-scatter.3.cloned.1.call-update) | async-done | bytes 917520 | tf_op jit(solution)/shard_map/reduce_scatter | solution.py:33
  153.9 0.2 dynamic-slice_reduce_fusion
  154.1 1.9 gather_fusion.6
  156.0 0.1 copy.41
  156.1 0.2 fusion.31
  156.4 0.2 fusion.33
  156.7 0.6 gather_fusion.3
  157.3 0.6 iota_reduce_fusion
  158.0 20.0 %reduce-scatter.5.cloned.1.call-done = bf16[32,3584]{1,0:T(8,128)(2,1)} async-done(((bf16[128,3584]{1,0:T(8,128)(2,1)}), bf16[32,3584]{1,0:T(8,128)(2,1)}) %reduce-scatter.5.cloned.1.call-update) | async-done | bytes 229392 | tf_op jit(solution)/shard_map/reduce_scatter | solution.py:33
  178.0 1.1 reshape.419
  179.1 0.6 gather_fusion.2
  179.9 3.2 collective-permute-start
  183.0 1.8 collective-permute-done
  184.8 0.2 broadcast_select_fusion
  185.0 1.4 collective-permute-start.1
  186.4 0.2 fusion.28
  186.6 3.3 collective-permute-done.1
  189.9 0.2 broadcast_select_fusion.1
  190.2 1.4 collective-permute-start.2
  191.8 0.1 broadcast_in_dim.75
  191.9 3.5 collective-permute-done.2
  195.4 0.2 broadcast_select_fusion.2
  195.7 0.7 gather_fusion.4
  196.4 0.7 gather_fusion.5
  197.1 0.2 gather.35
  197.3 0.8 select_convert_fusion
  198.1 0.1 reshape.427
  198.3 0.3 multiply_reduce_fusion
  198.6 3.0 convolution_convert_fusion
  201.6 7.0 %reshape.422 = bf16[128,4,3584]{2,1,0:T(4,128)(2,1)} reshape(bf16[512,3584]{1,0:T(8,128)(2,1)} %convolution_convert_fusion) | data formatting | bytes 7340032 | tf_op jit(solution)/shard_map/reshape | solution.py:139
  208.6 56.8 %all_to_all.27 = bf16[128,4,3584]{2,1,0:T(4,128)(2,1)} all-to-all(bf16[128,4,3584]{2,1,0:T(4,128)(2,1)} %reshape.422), channel_id=1, replica_groups=mesh['rep'=8,'ep_0'=4,'ep_1'=4] {'rep','ep_0','ep_1'}, dimensions={0} | all-to-all | bytes 7340032 | tf_op jit(solution)/shard_map/all_to_all | solution.py:138
  265.3 6.7 %reshape.423 = bf16[512,3584]{1,0:T(8,128)(2,1)} reshape(bf16[128,4,3584]{2,1,0:T(4,128)(2,1)} %all_to_all.27) | data formatting | bytes 7340032 | tf_op jit(solution)/shard_map/reshape | solution.py:147
  272.1 16.0 %fusion.7 = bf16[512,3584]{1,0:T(8,128)(2,1)} fusion(bf16[1,1024,3584]{2,1,0:T(8,128)(2,1)} %param.31, bf16[512,3584]{1,0:T(8,128)(2,1)} %reshape.423, bf16[1,3584,1024]{2,1,0:T(8,128)(2,1)} %param.30), kind=kOutput, calls=%fused_computation.19 | convolution fusion | flops 7520649216 | bytes 22020096 | tf_op jit(solution)/shard_map/dot_general | solution.py:152
  288.0 7.0 %reshape.424 = bf16[128,4,3584]{2,1,0:T(4,128)(2,1)} reshape(bf16[512,3584]{1,0:T(8,128)(2,1)} %fusion.7) | data formatting | bytes 7340032 | tf_op jit(solution)/shard_map/reshape | solution.py:156
  295.0 5.1 %all-to-all-start.2 = ((bf16[128,4,3584]{2,1,0:T(4,128)(2,1)}), bf16[128,4,3584]{2,1,0:T(4,128)(2,1)}, u32[]{:S(2)}, u32[]{:S(2)}) async-start(bf16[128,4,3584]{2,1,0:T(4,128)(2,1)} %reshape.424), calls=%async_computation.4 | async-start | bytes 7340032 | tf_op jit(solution)/shard_map/all_to_all | solution.py:155
  300.3 0.6 pad_clamp_fusion
  300.9 45.6 %all-to-all-done.2 = bf16[128,4,3584]{2,1,0:T(4,128)(2,1)} async-done(((bf16[128,4,3584]{2,1,0:T(4,128)(2,1)}), bf16[128,4,3584]{2,1,0:T(4,128)(2,1)}, u32[]{:S(2)}, u32[]{:S(2)}) %all-to-all-start.2) | async-done | bytes 3670048 | tf_op jit(solution)/shard_map/all_to_all | solution.py:155
  346.5 6.7 %reshape.425 = bf16[512,3584]{1,0:T(8,128)(2,1)} reshape(bf16[128,4,3584]{2,1,0:T(4,128)(2,1)} %all-to-all-done.2) | data formatting | bytes 7340032 | tf_op jit(solution)/shard_map/reshape | solution.py:163
  353.2 7.6 %gather_fusion.7 = bf16[256,3584]{1,0:T(8,128)(2,1)} fusion(bf16[512,3584]{1,0:T(8,128)(2,1)} %reshape.425, s32[1024]{0:T(1024)} %pad_clamp_fusion), kind=kCustom, calls=%fused_computation.7 | custom fusion | bytes 3671040 | tf_op jit(solution)/shard_map/gather | solution.py:163
  360.8 3.0 fusion.11
  363.7 1.8 add_convert_fusion
  365.5 1.8 reshape.426
  (59 shorter events, 1.2 us)
Async XLA Ops:
  7.2 8.3 %copy-start = (bf16[48,36864]{1,0:T(8,128)(2,1)S(1)}, bf16[48,36864]{1,0:T(8,128)(2,1)}, u32[]{:S(2)}) copy-start(bf16[48,36864]{1,0:T(8,128)(2,1)} %param.16) | copy-start | bytes 10616836
  7.2 146.7 %reduce-scatter.3.cloned.1.call-start = ((), (), s32[]{:S(2)}) async-start(), calls=%async_computation.5 | async-start | bytes 4587520 | tf_op jit(solution)/shard_map/reduce_scatter | solution.py:33
  40.5 3.4 copy-start.9
  40.5 3.4 copy-start.10
  66.7 37.5 %copy-start.13 = (bf16[4,512,128]{2,1,0:T(8,128)(2,1)S(1)}, bf16[4,512,128]{2,1,0:T(8,128)(2,1)}, u32[]{:S(2)}) copy-start(bf16[4,512,128]{2,1,0:T(8,128)(2,1)} %param.28) | copy-start | bytes 1572868
  104.1 2.7 copy-start.4
  110.7 43.3 %copy-start.11 = (s32[8,1,2]{0,2,1:T(2,128)S(1)}, s32[8,1,2]{0,2,1:T(2,128)}, u32[]{:S(2)}) copy-start(s32[8,1,2]{0,2,1:T(2,128)} %param.22) | copy-start | bytes 196
  110.7 43.4 %copy-start.2 = (s32[128]{0:T(128)S(1)}, s32[128]{0:T(128)}, u32[]{:S(2)}) copy-start(s32[128]{0:T(128)} %param.26) | copy-start | bytes 1540
  110.7 46.0 %copy-start.5 = (bf16[8,14336]{1,0:T(8,128)(2,1)S(1)}, bf16[8,14336]{1,0:T(8,128)(2,1)}, u32[]{:S(2)}) copy-start(bf16[8,14336]{1,0:T(8,128)(2,1)} %param.18) | copy-start | bytes 688132
  110.7 47.3 %copy-start.12 = (s32[1,2]{1,0:T(1,128)S(1)}, s32[1,2]{1,0:T(1,128)}, u32[]{:S(2)}) copy-start(s32[1,2]{1,0:T(1,128)} %param.23) | copy-start | bytes 28
  110.7 67.3 %reduce-scatter.5.cloned.1.call-start = ((), (), s32[]{:S(2)}) async-start(), calls=%async_computation.6 | async-start | bytes 1146880 | tf_op jit(solution)/shard_map/reduce_scatter | solution.py:33
  179.9 5.0 %collective-permute-start = (bf16[2,28672]{1,0:T(2,128)(2,1)S(1)}, bf16[2,28672]{1,0:T(2,128)(2,1)S(1)}, u32[]{:S(2)}, u32[]{:S(2)}) collective-permute-start(bf16[2,28672]{1,0:T(2,128)(2,1)S(1)} %constant_dynamic-update-slice_fusion), channel_id=1, source_target_pairs={{0,16},{16,32},{32,48},{48,64},{64,80},{80,96},{96,112},{112,0},{1... | collective-permute-start | bytes 344072 | tf_op jit(solution)/shard_map/ppermute | solution.py:27
  185.0 4.9 %collective-permute-start.1 = (bf16[2,28672]{1,0:T(2,128)(2,1)S(1)}, bf16[2,28672]{1,0:T(2,128)(2,1)S(1)}, u32[]{:S(2)}, u32[]{:S(2)}) collective-permute-start(bf16[2,28672]{1,0:T(2,128)(2,1)S(1)} %broadcast_select_fusion), channel_id=1, source_target_pairs={{0,32},{16,48},{32,64},{48,80},{64,96},{80,112},{96,0},{112,16},{1... | collective-permute-start | bytes 344072 | tf_op jit(solution)/shard_map/ppermute | solution.py:27
  190.2 5.2 %collective-permute-start.2 = (bf16[2,28672]{1,0:T(2,128)(2,1)S(1)}, bf16[2,28672]{1,0:T(2,128)(2,1)S(1)}, u32[]{:S(2)}, u32[]{:S(2)}) collective-permute-start(bf16[2,28672]{1,0:T(2,128)(2,1)S(1)} %broadcast_select_fusion.1), channel_id=1, source_target_pairs={{0,64},{16,80},{32,96},{48,112},{64,0},{80,16},{96,32},{112,48},{1... | collective-permute-start | bytes 344072 | tf_op jit(solution)/shard_map/ppermute | solution.py:27
  195.6 2.6 copy-start.6
  196.4 2.2 copy-start.7
  198.5 10.0 %copy-start.3 = (f32[32,3584]{1,0:T(8,128)}, f32[32,3584]{1,0:T(8,128)S(1)}, u32[]{:S(2)}) copy-start(f32[32,3584]{1,0:T(8,128)S(1)} %get-tuple-element.5) | copy-start | bytes 1376260
  295.0 5.1 %copy-start.8 = (f32[32,8]{0,1:T(8,128)S(1)}, f32[32,8]{0,1:T(8,128)}, u32[]{:S(2)}) copy-start(f32[32,8]{0,1:T(8,128)} %param.25) | copy-start | bytes 3076
  295.0 51.4 %all-to-all-start.2 = ((bf16[128,4,3584]{2,1,0:T(4,128)(2,1)}), bf16[128,4,3584]{2,1,0:T(4,128)(2,1)}, u32[]{:S(2)}, u32[]{:S(2)}) async-start(bf16[128,4,3584]{2,1,0:T(4,128)(2,1)} %reshape.424), calls=%async_computation.4 | async-start | bytes 7340032 | tf_op jit(solution)/shard_map/all_to_all | solution.py:155
  353.2 14.2 %copy-start.1 = (bf16[48,36864]{1,0:T(8,128)(2,1)S(1)}, bf16[48,36864]{1,0:T(8,128)(2,1)}, u32[]{:S(2)}) copy-start(bf16[48,36864]{1,0:T(8,128)(2,1)} %param.16) | copy-start | bytes 10616836
Sparse Core Ops, SparseCore 0:
  110.8 43.0 reduce-scatter.2
  156.3 21.6 reduce-scatter.4
where the time goes:
time: 376 us; the launch traced here: 374 us
  waiting for transfers between devices  117 us (31%)
  blocking collectives  91.4 us (24%)
  local copies, waits for them, and re-layouts  83 us (22%)
  matrix products  43.9 us (12%)
  between operations  14.3 us (4%)
  other arithmetic  13 us (3%)
  starting transfers between devices  11.2 us (3%)
    reduce_scatter x2, waiting for transfers between devices, own_rows_2(): so_far = lax.psum_scatter(so_far, axis, scatter_dimension=0, tiled=True)  63.1 us
    all_to_all x1, blocking collectives, per_device(): lax.all_to_all(outgoing_tokens.reshape(device_count, capacity, D), REP_EP...  56.8 us
    all_to_all x1, waiting for transfers between devices, per_device(): lax.all_to_all(outer_out.reshape(device_count, capacity, D), REP_EP, spli...  45.6 us
    all_to_all x1, blocking collectives, per_device(): lax.all_to_all(token_latent, EP, split_axis=1, concat_axis=0, tiled=True)  34.7 us
    dot_general x1, matrix products, per_device(): jnp.dot(inner_act, expert_out[0], preferred_element_type=jnp.float32)  16 us
    another operation x1, local copies, waits for them, and re-layouts, attend(): key_rows = key_block.reshape(request_count, MAXP * PAGE, KVW)  14.2 us
    sub x1, matrix products, attend(): exponent = jnp.exp(scores - jnp.max(scores, axis=2, keepdims=True))  10.7 us
    ppermute x3, waiting for transfers between devices, shifted(): return lax.ppermute(value, axis, pairs)  8.65 us
  transfers between devices with their start and end apart: 6, of which 6 were waited for; matrix products, arithmetic and copies ran while one was open for 1% of the time, Pallas kernels for 0%

commit v1 on v0

--- a/solution.py
+++ b/solution.py
@@ -98,7 +98,10 @@
     tokens_dev = REQ_DEV * SPEC
     heads_dev = value_up.shape[0]
     token_latent = own_latent.reshape(tokens_dev, HEADS * LAT)
-    regrouped = lax.all_to_all(token_latent, EP, split_axis=1, concat_axis=0, tiled=True)
+    regrouped = jnp.concatenate(
+        lax.all_to_all(jnp.stack(jnp.split(token_latent, lax.axis_size(EP), axis=1)), EP, 0, 0),
+        axis=0,
+    )
     row_block = regrouped.reshape(tokens_dev * lax.axis_size(EP), heads_dev, LAT)
     lifted = jnp.einsum(
         "thl,hlv->thv", row_block, value_up, preferred_element_type=jnp.float32

time: 376 us -> 373 us (level)
    another operation x3 -> x6, local copies, waits for them, and re-layouts: 0.02 us -> 5.68 us  [the longest x1 2.87 us: per_device(): token_latent = own_latent.reshape(tokens_dev, HEADS * LAT)]
    all_to_all x2 -> x0, local copies, waits for them, and re-layouts: 4.25 us -> none  [per_device(): lax.all_to_all(token_latent, EP, split_axis=1, concat_axis=0, tiled=True)]
where the time goes in v1:
time: 373 us; the launch traced here: 372 us
  waiting for transfers between devices  117 us (31%)
  blocking collectives  91.3 us (24%)
  local copies, waits for them, and re-layouts  81.4 us (22%)
  matrix products  43.9 us (12%)
  between operations  14.5 us (4%)
  other arithmetic  11.7 us (3%)
  starting transfers between devices  11.3 us (3%)
    reduce_scatter x2, waiting for transfers between devices, own_rows_2(): so_far = lax.psum_scatter(so_far, axis, scatter_dimension=0, tiled=True)  63.1 us
    all_to_all x1, blocking collectives, per_device(): lax.all_to_all(outgoing_tokens.reshape(device_count, capacity, D), REP_EP...  56.8 us
    all_to_all x1, waiting for transfers between devices, per_device(): lax.all_to_all(outer_out.reshape(device_count, capacity, D), REP_EP, spli...  45.6 us
    all_to_all x1, blocking collectives, per_device(): lax.all_to_all(jnp.stack(jnp.split(token_latent, lax.axis_size(EP), axis=...  34.5 us
    dot_general x1, matrix products, per_device(): jnp.dot(inner_act, expert_out[0], preferred_element_type=jnp.float32)  16 us
    another operation x1, local copies, waits for them, and re-layouts, attend(): key_rows = key_block.reshape(request_count, MAXP * PAGE, KVW)  14.2 us
    sub x1, matrix products, attend(): exponent = jnp.exp(scores - jnp.max(scores, axis=2, keepdims=True))  10.7 us
    ppermute x3, waiting for transfers between devices, shifted(): return lax.ppermute(value, axis, pairs)  8.66 us
  transfers between devices with their start and end apart: 6, of which 6 were waited for; matrix products, arithmetic and copies ran while one was open for 1% of the time, Pallas kernels for 0%

profile of v1, /device:TPU:1, one launch (start us, length us, event | category | flops | bytes accessed | tf_op | source)
XLA Modules:
  0.0 371.6 jit_solution(14457541736659279521)
XLA Ops:
  7.2 0.6 and_select_fusion
  7.8 1.3 fusion.61
  9.1 0.2 reduce-window.18
  9.3 0.7 bitcast_subtract_fusion.1
  10.1 1.2 gather_fusion
  11.5 0.7 reshape.430
  12.1 0.8 copy.38
  12.9 0.7 reshape.411
  13.6 0.7 compare_select_fusion.3
  14.2 0.7 pad_clamp_fusion.1
  14.9 8.1 %gather_fusion.1 = bf16[96,36864]{1,0:T(8,128)(2,1)} fusion(bf16[48,36864]{1,0:T(8,128)(2,1)S(1)} %copy-done, s32[1024]{0:T(1024)S(1)} %get-tuple-element.18), kind=kCustom, calls=%fused_computation.1 | custom fusion | bytes 14156160 | tf_op jit(solution)/shard_map/gather | solution.py:90
  23.0 14.2 %reshape_reshape.9 = bf16[8,768,576]{2,1,0:T(8,128)(2,1)} reshape(bf16[96,36864]{1,0:T(8,128)(2,1)} %gather_fusion.1) | data formatting | bytes 14155776 | tf_op jit(solution)/shard_map/reshape;reshape | solution.py:39
  37.2 2.7 reshape.492
  40.0 3.3 reshape.408
  43.4 10.7 %fusion.67 = (f32[8,256]{1,0:T(8,128)S(1)}, f32[8,256,768]{1,2,0:T(8,128)}) fusion(s32[8,256]{1,0:T(8,128)S(1)} %broadcast_add_fusion.1, bf16[8,768,576]{2,1,0:T(8,128)(2,1)} %reshape_reshape.9, bf16[8,256,576]{2,1,0:T(8,128)(2,1)} %reshape.408), kind=kOutput, calls=%fused_computation.147 | convolution fusion | flops 1819804416 | bytes 15745024 | tf_op jit(solution)/shard_map/sub | solution.py:50
  54.0 7.8 %fusion.18 = bf16[8,256,512]{2,1,0:T(8,128)(2,1)} fusion(bf16[8,768,576]{2,1,0:T(8,128)(2,1)} %reshape_reshape.9, f32[8,256,768]{1,2,0:T(8,128)} %get-tuple-element.16, f32[8,256]{1,0:T(8,128)S(1)} %get-tuple-element.15), kind=kOutput, calls=%fused_computation.32 | convolution fusion | flops 1614807040 | bytes 14688256 | tf_op jit(solution)/shard_map/rqk,rkl->rql/dot_general | solution.py:52
  61.8 2.9 reshape_reshape.10
  65.0 34.5 %all_to_all.15 = bf16[16,32,2048]{2,1,0:T(8,128)(2,1)S(1)} all-to-all(bf16[16,32,2048]{2,1,0:T(8,128)(2,1)S(1)} %fusion.32), channel_id=1, replica_groups=mesh['rep'=8,'ep_0'=4,'ep_1'=4] {'ep_0','ep_1'}, dimensions={0} | all-to-all | bytes 4194304 | tf_op jit(solution)/shard_map/all_to_all | solution.py:102
  99.6 2.8 reshape_reshape.11
  102.3 2.6 fusion.23
  105.0 3.9 %convolution_convert_fusion.1 = bf16[512,3584]{1,0:T(8,128)(2,1)} fusion(bf16[512,512]{0,1:T(8,128)(2,1)S(1)} %bitcast.165, bf16[512,3584]{1,0:T(8,128)(2,1)S(1)} %copy-done.6), kind=kOutput, calls=%fused_computation.21 | convolution fusion | flops 1880883200 | bytes 7864320 | tf_op jit(solution)/shard_map/dot_general | solution.py:110
  109.0 43.1 %reduce-scatter.3.cloned.1.call-done = bf16[128,3584]{1,0:T(8,128)(2,1)} async-done(((bf16[512,3584]{1,0:T(8,128)(2,1)}), bf16[128,3584]{1,0:T(8,128)(2,1)}) %reduce-scatter.3.cloned.1.call-update) | async-done | bytes 917520 | tf_op jit(solution)/shard_map/reduce_scatter | solution.py:33
  152.1 0.2 dynamic-slice_reduce_fusion
  152.3 1.9 gather_fusion.6
  154.2 0.1 copy.39
  154.3 0.2 fusion.31
  154.6 0.2 fusion.49
  154.9 0.6 gather_fusion.3
  155.6 0.6 iota_reduce_fusion
  156.2 20.0 %reduce-scatter.5.cloned.1.call-done = bf16[32,3584]{1,0:T(8,128)(2,1)} async-done(((bf16[128,3584]{1,0:T(8,128)(2,1)}), bf16[32,3584]{1,0:T(8,128)(2,1)}) %reduce-scatter.5.cloned.1.call-update) | async-done | bytes 229392 | tf_op jit(solution)/shard_map/reduce_scatter | solution.py:33
  176.2 1.1 reshape.410
  177.4 0.6 gather_fusion.2
  178.1 3.1 collective-permute-start
  181.2 1.8 collective-permute-done
  183.0 0.2 broadcast_select_fusion
  183.2 1.3 collective-permute-start.1
  184.6 0.2 fusion.28
  184.8 3.3 collective-permute-done.1
  188.2 0.2 broadcast_select_fusion.1
  188.4 1.7 collective-permute-start.2
  190.0 0.1 fusion.52
  190.2 0.1 broadcast_in_dim.75
  190.3 3.5 collective-permute-done.2
  193.8 0.2 broadcast_select_fusion.2
  194.1 0.7 gather_fusion.4
  194.8 0.7 gather_fusion.5
  195.5 0.2 gather.35
  195.7 0.8 select_convert_fusion
  196.6 0.1 reshape.418
  196.7 0.3 multiply_reduce_fusion
  197.0 3.0 convolution_convert_fusion
  200.0 7.0 %reshape.413 = bf16[128,4,3584]{2,1,0:T(4,128)(2,1)} reshape(bf16[512,3584]{1,0:T(8,128)(2,1)} %convolution_convert_fusion) | data formatting | bytes 7340032 | tf_op jit(solution)/shard_map/reshape | solution.py:142
  207.0 56.8 %all_to_all.16 = bf16[128,4,3584]{2,1,0:T(4,128)(2,1)} all-to-all(bf16[128,4,3584]{2,1,0:T(4,128)(2,1)} %reshape.413), channel_id=1, replica_groups=mesh['rep'=8,'ep_0'=4,'ep_1'=4] {'rep','ep_0','ep_1'}, dimensions={0} | all-to-all | bytes 7340032 | tf_op jit(solution)/shard_map/all_to_all | solution.py:141
  263.8 6.7 %reshape.414 = bf16[512,3584]{1,0:T(8,128)(2,1)} reshape(bf16[128,4,3584]{2,1,0:T(4,128)(2,1)} %all_to_all.16) | data formatting | bytes 7340032 | tf_op jit(solution)/shard_map/reshape | solution.py:150
  270.5 16.0 %fusion.7 = bf16[512,3584]{1,0:T(8,128)(2,1)} fusion(bf16[1,1024,3584]{2,1,0:T(8,128)(2,1)} %param.31, bf16[512,3584]{1,0:T(8,128)(2,1)} %reshape.414, bf16[1,3584,1024]{2,1,0:T(8,128)(2,1)} %param.30), kind=kOutput, calls=%fused_computation.19 | convolution fusion | flops 7520649216 | bytes 22020096 | tf_op jit(solution)/shard_map/dot_general | solution.py:155
  286.5 7.0 %reshape.415 = bf16[128,4,3584]{2,1,0:T(4,128)(2,1)} reshape(bf16[512,3584]{1,0:T(8,128)(2,1)} %fusion.7) | data formatting | bytes 7340032 | tf_op jit(solution)/shard_map/reshape | solution.py:159
  293.5 5.1 %all-to-all-start.2 = ((bf16[128,4,3584]{2,1,0:T(4,128)(2,1)}), bf16[128,4,3584]{2,1,0:T(4,128)(2,1)}, u32[]{:S(2)}, u32[]{:S(2)}) async-start(bf16[128,4,3584]{2,1,0:T(4,128)(2,1)} %reshape.415), calls=%async_computation.4 | async-start | bytes 7340032 | tf_op jit(solution)/shard_map/all_to_all | solution.py:158
  298.6 0.6 pad_clamp_fusion
  299.2 45.6 %all-to-all-done.2 = bf16[128,4,3584]{2,1,0:T(4,128)(2,1)} async-done(((bf16[128,4,3584]{2,1,0:T(4,128)(2,1)}), bf16[128,4,3584]{2,1,0:T(4,128)(2,1)}, u32[]{:S(2)}, u32[]{:S(2)}) %all-to-all-start.2) | async-done | bytes 3670048 | tf_op jit(solution)/shard_map/all_to_all | solution.py:158
  344.9 6.7 %reshape.416 = bf16[512,3584]{1,0:T(8,128)(2,1)} reshape(bf16[128,4,3584]{2,1,0:T(4,128)(2,1)} %all-to-all-done.2) | data formatting | bytes 7340032 | tf_op jit(solution)/shard_map/reshape | solution.py:166
  351.6 7.6 %gather_fusion.7 = bf16[256,3584]{1,0:T(8,128)(2,1)} fusion(bf16[512,3584]{1,0:T(8,128)(2,1)} %reshape.416, s32[1024]{0:T(1024)} %pad_clamp_fusion), kind=kCustom, calls=%fused_computation.7 | custom fusion | bytes 3671040 | tf_op jit(solution)/shard_map/gather | solution.py:166
  359.2 3.0 fusion.11
  362.2 0.7 add_convert_fusion
  362.9 1.8 reshape.417
  (78 shorter events, 1.3 us)
Async XLA Ops:
  7.2 7.8 %copy-start = (bf16[48,36864]{1,0:T(8,128)(2,1)S(1)}, bf16[48,36864]{1,0:T(8,128)(2,1)}, u32[]{:S(2)}) copy-start(bf16[48,36864]{1,0:T(8,128)(2,1)} %param.16) | copy-start | bytes 10616836
  7.2 3.0 copy-start.2
  7.2 144.9 %reduce-scatter.3.cloned.1.call-start = ((), (), s32[]{:S(2)}) async-start(), calls=%async_computation.5 | async-start | bytes 4587520 | tf_op jit(solution)/shard_map/reduce_scatter | solution.py:33
  39.9 3.4 copy-start.11
  39.9 3.4 copy-start.12
  99.6 2.8 copy-start.15
  102.3 2.7 copy-start.6
  108.9 43.2 %copy-start.13 = (s32[8,1,2]{0,2,1:T(2,128)S(1)}, s32[8,1,2]{0,2,1:T(2,128)}, u32[]{:S(2)}) copy-start(s32[8,1,2]{0,2,1:T(2,128)} %param.22) | copy-start | bytes 196
  108.9 43.4 %copy-start.3 = (s32[128]{0:T(128)S(1)}, s32[128]{0:T(128)}, u32[]{:S(2)}) copy-start(s32[128]{0:T(128)} %param.26) | copy-start | bytes 1540
  108.9 46.0 %copy-start.7 = (bf16[8,14336]{1,0:T(8,128)(2,1)S(1)}, bf16[8,14336]{1,0:T(8,128)(2,1)}, u32[]{:S(2)}) copy-start(bf16[8,14336]{1,0:T(8,128)(2,1)} %param.18) | copy-start | bytes 688132
  108.9 47.2 %copy-start.14 = (s32[1,2]{1,0:T(1,128)S(1)}, s32[1,2]{1,0:T(1,128)}, u32[]{:S(2)}) copy-start(s32[1,2]{1,0:T(1,128)} %param.23) | copy-start | bytes 28
  108.9 67.3 %reduce-scatter.5.cloned.1.call-start = ((), (), s32[]{:S(2)}) async-start(), calls=%async_computation.6 | async-start | bytes 1146880 | tf_op jit(solution)/shard_map/reduce_scatter | solution.py:33
  178.1 4.9 %collective-permute-start = (bf16[2,28672]{1,0:T(2,128)(2,1)S(1)}, bf16[2,28672]{1,0:T(2,128)(2,1)S(1)}, u32[]{:S(2)}, u32[]{:S(2)}) collective-permute-start(bf16[2,28672]{1,0:T(2,128)(2,1)S(1)} %constant_dynamic-update-slice_fusion), channel_id=1, source_target_pairs={{0,16},{16,32},{32,48},{48,64},{64,80},{80,96},{96,112},{112,0},{1... | collective-permute-start | bytes 344072 | tf_op jit(solution)/shard_map/ppermute | solution.py:27
  183.2 4.9 %collective-permute-start.1 = (bf16[2,28672]{1,0:T(2,128)(2,1)S(1)}, bf16[2,28672]{1,0:T(2,128)(2,1)S(1)}, u32[]{:S(2)}, u32[]{:S(2)}) collective-permute-start(bf16[2,28672]{1,0:T(2,128)(2,1)S(1)} %broadcast_select_fusion), channel_id=1, source_target_pairs={{0,32},{16,48},{32,64},{48,80},{64,96},{80,112},{96,0},{112,16},{1... | collective-permute-start | bytes 344072 | tf_op jit(solution)/shard_map/ppermute | solution.py:27
  188.4 5.4 %collective-permute-start.2 = (bf16[2,28672]{1,0:T(2,128)(2,1)S(1)}, bf16[2,28672]{1,0:T(2,128)(2,1)S(1)}, u32[]{:S(2)}, u32[]{:S(2)}) collective-permute-start(bf16[2,28672]{1,0:T(2,128)(2,1)S(1)} %broadcast_select_fusion.1), channel_id=1, source_target_pairs={{0,64},{16,80},{32,96},{48,112},{64,0},{80,16},{96,32},{112,48},{1... | collective-permute-start | bytes 344072 | tf_op jit(solution)/shard_map/ppermute | solution.py:27
  194.8 1.9 copy-start.8
  195.5 1.5 copy-start.9
  197.0 10.0 %copy-start.4 = (f32[32,3584]{1,0:T(8,128)}, f32[32,3584]{1,0:T(8,128)S(1)}, u32[]{:S(2)}) copy-start(f32[32,3584]{1,0:T(8,128)S(1)} %get-tuple-element.5) | copy-start | bytes 1376260
  293.5 5.1 %copy-start.10 = (f32[32,8]{0,1:T(8,128)S(1)}, f32[32,8]{0,1:T(8,128)}, u32[]{:S(2)}) copy-start(f32[32,8]{0,1:T(8,128)} %param.25) | copy-start | bytes 3076
  293.5 51.4 %all-to-all-start.2 = ((bf16[128,4,3584]{2,1,0:T(4,128)(2,1)}), bf16[128,4,3584]{2,1,0:T(4,128)(2,1)}, u32[]{:S(2)}, u32[]{:S(2)}) async-start(bf16[128,4,3584]{2,1,0:T(4,128)(2,1)} %reshape.415), calls=%async_computation.4 | async-start | bytes 7340032 | tf_op jit(solution)/shard_map/all_to_all | solution.py:158
  351.6 13.2 %copy-start.1 = (bf16[48,36864]{1,0:T(8,128)(2,1)S(1)}, bf16[48,36864]{1,0:T(8,128)(2,1)}, u32[]{:S(2)}) copy-start(bf16[48,36864]{1,0:T(8,128)(2,1)} %param.16) | copy-start | bytes 10616836
  359.2 3.0 copy-start.5
Sparse Core Ops, SparseCore 0:
  109.0 43.0 reduce-scatter.2
  154.5 21.6 reduce-scatter.4
